TPU v7x, 256 devices: a whole 4x4x8 slice. The times are simulated.
256 devices in a mesh: gz: 64 (over x, z_hi, y), xy: 4 (over z_lo, core).
Axes of the slice: x: 4, y: 4, z: 8 (z_hi: 4, z_lo: 2; z = z_hi * 2 + z_lo), core: 2. Of those that a mesh axis runs over, the one named last changes fastest.
Arguments:
- patches: bfloat16 [64, 8, 16, 128, 128], P('gz', 'xy'), may hold values from -6 to 6
- peak_offsets: int32 [64, 6, 8, 16], P('gz', None, 'xy'), may hold values from -4 to 4
- valid_masks: int32 [64, 3, 8, 16], P('gz', None, 'xy'), may hold values 0 or 1
- initial_positions: float32 [2, 64, 128, 256], P(None, 'gz', 'xy'), may hold values from -40 to 40
Outputs:
- positions: float32 [2, 64, 128, 256], P(None, 'gz', 'xy')
- targets: float32 [64, 6, 8, 16], P('gz', None, 'xy')
- surfaces: bfloat16 [64, 3, 8, 16, 128, 128], P('gz', None, 'xy')
- force_rms: float32 [4], replicated
All inputs are finite; a program needn't handle non-finite values. No bound on the sum of `valid_masks` on one device may be relied on, other than what follows from the above.
Results may differ from a plain program's by a relative error of at most 0.0091.
Values may be sent and summed in bfloat16 or wider, within the bound.
A program may use at most 64 MiB of HBM per device.

v0:
```python
import math
import jax
import jax.numpy as jnp
from jax import lax
from jax.sharding import Mesh
from jax.sharding import PartitionSpec as P

SUB = 16
ITERS = 4
GZ = ("gz_0", "gz_1", "gz_2")
XY = ("xy_0", "xy_1")
GZ_XY = ("gz_0", "gz_1", "gz_2", "xy_0", "xy_1")
lattice_stiff = 0.5
clip_level = 5.0
step_size = 0.2
floor_ratio = 0.4
tiny_eps = 1e-06


def from_behind(array, axis, by):
    count = lax.axis_size(axis)
    pairs = [(i, i + by) for i in range(count) if 0 <= i + by < count]
    return lax.ppermute(array, axis, pairs)


def extended(block, sides, width):
    for axis, dim in sides:
        count = lax.axis_size(axis)
        forward = [(i, i + 1) for i in range(count - 1)]
        backward = [(target, source) for source, target in forward]
        low = lax.ppermute(
            lax.slice_in_dim(block, block.shape[dim] - width, None, axis=dim), axis, forward
        )
        high = lax.ppermute(lax.slice_in_dim(block, 0, width, axis=dim), axis, backward)
        block = jnp.concatenate([low, block, high], axis=dim)
    return block


def over_axes(array, axes):
    for axis in axes:
        array = lax.psum(array, axis)
    return array


def dft_tables(length):
    series = jnp.arange(length, dtype=jnp.int32)
    product = series[:, None] * series[None, :] % length
    angles = 2.0 * math.pi / length * product.astype(jnp.float32)
    return (jnp.cos(angles).astype(jnp.bfloat16), jnp.sin(angles).astype(jnp.bfloat16))


def right_product(left, table):
    return jnp.einsum("pab,bk->pak", left, table, preferred_element_type=jnp.float32)


def left_product(table, right):
    return jnp.einsum("ja,pak->pjk", table, right, preferred_element_type=jnp.float32)


def spectrum(tiles, cosine, sine):
    row_cos = right_product(tiles, cosine).astype(jnp.bfloat16)
    row_sin = right_product(tiles, sine).astype(jnp.bfloat16)
    real = left_product(cosine, row_cos) - left_product(sine, row_sin)
    imag = -(left_product(sine, row_cos) + left_product(cosine, row_sin))
    return (real, imag)


def correlate(first, second, cosine, sine, length):
    cross_real = (first[0] * second[0] + first[1] * second[1]).astype(jnp.bfloat16)
    cross_imag = (first[0] * second[1] - first[1] * second[0]).astype(jnp.bfloat16)
    half_real = (right_product(cross_real, cosine) - right_product(cross_imag, sine)).astype(
        jnp.bfloat16
    )
    half_imag = (right_product(cross_real, sine) + right_product(cross_imag, cosine)).astype(
        jnp.bfloat16
    )
    whole = left_product(cosine, half_real) - left_product(sine, half_imag)
    return whole / float(length * length)


def refine(corr, shift_rows, shift_cols, length):
    series = jnp.arange(length, dtype=jnp.int32)
    taps = jnp.arange(3, dtype=jnp.int32) - 1
    row_index = (shift_rows[:, None] + taps[None, :] + length) % length
    col_index = (shift_cols[:, None] + taps[None, :] + length) % length
    row_pick = (series[None, None, :] == row_index[:, :, None]).astype(jnp.float32)
    col_pick = (series[None, None, :] == col_index[:, :, None]).astype(jnp.float32)
    partial_rows = jnp.einsum("pta,pab->ptb", row_pick, corr)
    values = jnp.einsum("ptb,psb->pts", partial_rows, col_pick)
    floor_value = floor_ratio * length
    along_rows = values[:, :, 1]
    along_cols = values[:, 1, :]
    sub_rows = (along_rows[:, 2] - along_rows[:, 0]) / jnp.maximum(
        jnp.sum(jnp.abs(along_rows), axis=1), floor_value
    )
    sub_cols = (along_cols[:, 2] - along_cols[:, 0]) / jnp.maximum(
        jnp.sum(jnp.abs(along_cols), axis=1), floor_value
    )
    return (shift_rows.astype(jnp.float32) + sub_rows, shift_cols.astype(jnp.float32) + sub_cols)


def expand_nodes(array, axis):
    return jnp.repeat(jnp.repeat(array, SUB, axis=axis), SUB, axis=axis + 1)


def local(patches, peak_offsets, valid_masks, initial_positions):
    length = patches.shape[-1]
    rows_dev = patches.shape[1]
    columns = patches.shape[2]
    tiles_count = rows_dev * columns
    cosine, sine = dft_tables(length)
    own = spectrum(patches.reshape(tiles_count, length, length), cosine, sine)
    offsets = peak_offsets.reshape(6, tiles_count)
    results = []
    maps = []
    for distance in range(1, 4):
        other_tiles = from_behind(patches, GZ, -distance)
        other = spectrum(other_tiles.reshape(tiles_count, length, length), cosine, sine)
        corr = correlate(own, other, cosine, sine, length)
        maps.append(corr.astype(jnp.bfloat16).reshape(rows_dev, columns, length, length))
        rows_target, cols_target = refine(
            corr, offsets[2 * distance - 2], offsets[2 * distance - 1], length
        )
        results.append(rows_target)
        results.append(cols_target)
    targets = jnp.stack(results).reshape(1, 6, rows_dev, columns)
    surfaces = jnp.stack(maps).reshape(1, 3, rows_dev, columns, length, length)
    depth_count = lax.axis_size(GZ)
    depth_index = lax.axis_index(GZ)
    tile_index = lax.axis_index(XY)
    tile_count = lax.axis_size(XY)
    weights = []
    vectors = []
    lower_weights = []
    lower_vectors = []
    for distance in range(1, 4):
        live = (depth_index + distance < depth_count).astype(jnp.float32)
        weight = valid_masks[:, distance - 1].astype(jnp.float32) * (1.0 / distance) * live
        vector = jnp.stack([targets[:, 2 * distance - 2], targets[:, 2 * distance - 1]], axis=0)
        vector_low, weight_low = from_behind((vector, weight), GZ, distance)
        weights.append(expand_nodes(weight, 1))
        vectors.append(expand_nodes(vector, 2))
        lower_weights.append(expand_nodes(weight_low, 1))
        lower_vectors.append(expand_nodes(vector_low, 2))
    count = 2.0 * depth_count * tile_count * initial_positions.shape[2] * initial_positions.shape[3]
    positions = initial_positions
    norms = []
    for iteration in range(ITERS):
        padded = extended(positions.astype(jnp.bfloat16), ((XY, 2),), 1).astype(positions.dtype)
        top_row = jnp.where(tile_index == 0, positions[:, :, :1], padded[:, :, :1])
        bottom_row = jnp.where(
            tile_index == tile_count - 1, positions[:, :, -1:], padded[:, :, -1:]
        )
        upper_rows = jnp.concatenate([top_row, positions[:, :, :-1]], axis=2)
        lower_rows = jnp.concatenate([positions[:, :, 1:], bottom_row], axis=2)
        edged = jnp.pad(positions, ((0, 0), (0, 0), (0, 0), (1, 1)), mode="edge")
        lattice = (
            upper_rows + lower_rows + edged[:, :, :, :-2] + edged[:, :, :, 2:] - 4.0 * positions
        )
        force = lattice_stiff * lattice
        climbing = positions
        sinking = positions
        for distance in range(1, 4):
            climbing = from_behind(climbing.astype(jnp.bfloat16), GZ, -1).astype(climbing.dtype)
            sinking = from_behind(sinking.astype(jnp.bfloat16), GZ, 1).astype(sinking.dtype)
            force = force + weights[distance - 1] * (climbing - positions - vectors[distance - 1])
            force = force - lower_weights[distance - 1] * (
                positions - sinking - lower_vectors[distance - 1]
            )
        total = over_axes(jnp.sum(force * force), GZ_XY)
        rms = jnp.sqrt(total / count + tiny_eps)
        factor = jnp.minimum(1.0, clip_level / rms)
        positions = positions + step_size * factor * force
        norms.append(rms)
    return (positions, targets, surfaces, jnp.stack(norms))


def solution(mesh):
    split = Mesh(mesh.devices.reshape(4, 4, 4, 2, 2), ("gz_0", "gz_1", "gz_2", "xy_0", "xy_1"))
    placed = (
        P(GZ, XY, None, None, None),
        P(GZ, None, XY, None),
        P(GZ, None, XY, None),
        P(None, GZ, XY, None),
    )
    return jax.shard_map(
        local,
        mesh=split,
        in_specs=placed,
        out_specs=(
            P(None, GZ, XY, None),
            P(GZ, None, XY, None),
            P(GZ, None, XY, None, None, None),
            P(),
        ),
        check_vma=False,
    )
```

profile of v0, /device:TPU:1, one launch (start us, length us, event | category | flops | bytes accessed | tf_op | source)
XLA Modules:
  0.0 543.9 jit_solution(4362355122713396732)
XLA Ops:
  6.1 5.2 collective-permute-start.5
  25.6 10.0 %collective-permute-start.9 = (f32[1,2,16]{2,1,0:T(2,128)S(1)}, f32[1,2,16]{2,1,0:T(2,128)S(1)}, u32[]{:S(2)}, u32[]{:S(2)}) collective-permute-start(f32[1,2,16]{2,1,0:T(2,128)S(1)} %get-tuple-element.92), channel_id=1, source_target_pairs={{0,8},{4,12},{8,16},{12,20},{16,24},{20,28},{24,32},{28,36},{32,40... | collective-permute-start | bytes 392 | tf_op jit(solution)/shard_map/ppermute | solution.py:23
  36.4 6.4 %collective-permute-start.14 = (f32[1,2,16]{2,1,0:T(2,128)S(1)}, f32[1,2,16]{2,1,0:T(2,128)S(1)}, u32[]{:S(2)}, u32[]{:S(2)}) collective-permute-start(f32[1,2,16]{2,1,0:T(2,128)S(1)} %get-tuple-element.91), channel_id=1, source_target_pairs={{0,12},{4,16},{8,20},{12,24},{16,28},{20,32},{24,36},{28,40},{32,4... | collective-permute-start | bytes 392 | tf_op jit(solution)/shard_map/ppermute | solution.py:23
  43.4 29.5 %collective-permute-start = (bf16[2,1,1,256]{3,2,1,0:T(2,128)(2,1)S(1)}, bf16[2,1,1,256]{3,2,1,0:T(2,128)(2,1)S(1)}, u32[]{:S(2)}, u32[]{:S(2)}) collective-permute-start(bf16[2,1,1,256]{3,2,1,0:T(2,128)(2,1)S(1)} %get-tuple-element.82), channel_id=1, source_target_pairs={{0,1},{1,2},{2,3},{4,5},{5,6},{6,7},{8,9},{9,10},{10,11},{12,13},{... | collective-permute-start | bytes 3080 | tf_op jit(solution)/shard_map/ppermute | solution.py:31
  81.9 6.0 %collective-permute-start.10 = (bf16[2,1,32,256]{3,2,1,0:T(8,128)(2,1)}, bf16[2,1,32,256]{3,2,1,0:T(8,128)(2,1)}, u32[]{:S(2)}, u32[]{:S(2)}) collective-permute-start(bf16[2,1,32,256]{3,2,1,0:T(8,128)(2,1)} %collective-permute-done.5), channel_id=1, source_target_pairs={{0,4},{4,8},{8,12},{12,16},{16,20},{20,24},{24,28},{28,32},{32,36}... | collective-permute-start | bytes 98312 | tf_op jit(solution)/shard_map/ppermute | solution.py:23
  88.4 34.0 %collective-permute-done.7 = bf16[2,1,32,256]{3,2,1,0:T(8,128)(2,1)} collective-permute-done((bf16[2,1,32,256]{3,2,1,0:T(8,128)(2,1)}, bf16[2,1,32,256]{3,2,1,0:T(8,128)(2,1)}, u32[]{:S(2)}, u32[]{:S(2)}) %collective-permute-start.7) | collective-permute-done | bytes 32800 | tf_op jit(solution)/shard_map/ppermute | solution.py:23
  199.1 6.8 %collective-permute-start.6 = (f32[2,1,2,16]{3,2,1,0:T(2,128)S(1)}, f32[2,1,2,16]{3,2,1,0:T(2,128)S(1)}, u32[]{:S(2)}, u32[]{:S(2)}) collective-permute-start(f32[2,1,2,16]{3,2,1,0:T(2,128)S(1)} %get-tuple-element.97), channel_id=1, source_target_pairs={{0,4},{4,8},{8,12},{12,16},{16,20},{20,24},{24,28},{28,32},{32,36}... | collective-permute-start | bytes 776 | tf_op jit(solution)/shard_map/ppermute | solution.py:23
  207.0 25.7 %collective-permute-start.11 = (f32[2,1,2,16]{3,2,1,0:T(2,128)S(1)}, f32[2,1,2,16]{3,2,1,0:T(2,128)S(1)}, u32[]{:S(2)}, u32[]{:S(2)}) collective-permute-start(f32[2,1,2,16]{3,2,1,0:T(2,128)S(1)} %get-tuple-element.99), channel_id=1, source_target_pairs={{0,8},{4,12},{8,16},{12,20},{16,24},{20,28},{24,32},{28,36},{32,40... | collective-permute-start | bytes 776 | tf_op jit(solution)/shard_map/ppermute | solution.py:23
  240.9 20.3 %psum.140 = f32[]{:T(128)} all-reduce(f32[]{:T(128)} %get-tuple-element.40), channel_id=1, replica_groups=mesh['gz_0'=4,'gz_1'=4,'gz_2'=4,'xy_0'=2,'xy_1'=2] {'gz_0'}, use_global_device_ids=true, to_apply=%region_7.8 | all-reduce | flops 1 | bytes 8 | tf_op jit(solution)/shard_map/psum | solution.py:41
  261.1 9.2 %psum.141 = f32[]{:T(128)} all-reduce(f32[]{:T(128)} %psum.140), channel_id=1, replica_groups=mesh['gz_0'=4,'gz_1'=4,'gz_2'=4,'xy_0'=2,'xy_1'=2] {'gz_1'}, use_global_device_ids=true, to_apply=%region_8.9 | all-reduce | flops 1 | bytes 8 | tf_op jit(solution)/shard_map/psum | solution.py:41
  270.4 6.6 %psum.142 = f32[]{:T(128)} all-reduce(f32[]{:T(128)} %psum.141), channel_id=1, replica_groups=mesh['gz_0'=4,'gz_1'=4,'gz_2'=4,'xy_0'=2,'xy_1'=2] {'gz_2'}, use_global_device_ids=true, to_apply=%region_9.10 | all-reduce | flops 1 | bytes 8 | tf_op jit(solution)/shard_map/psum | solution.py:41
  281.7 10.7 %psum.144 = f32[]{:T(128)} all-reduce(f32[]{:T(128)} %psum.143), channel_id=1, replica_groups=mesh['gz_0'=4,'gz_1'=4,'gz_2'=4,'xy_0'=2,'xy_1'=2] {'xy_1'}, use_global_device_ids=true, to_apply=%region_11.12 | all-reduce | flops 1 | bytes 8 | tf_op jit(solution)/shard_map/psum | solution.py:41
  315.5 24.1 %psum.145 = f32[]{:T(128)} all-reduce(f32[]{:T(128)} %get-tuple-element.36), channel_id=1, replica_groups=mesh['gz_0'=4,'gz_1'=4,'gz_2'=4,'xy_0'=2,'xy_1'=2] {'gz_0'}, use_global_device_ids=true, to_apply=%region_13.14 | all-reduce | flops 1 | bytes 8 | tf_op jit(solution)/shard_map/psum | solution.py:41
  339.6 7.5 %psum.146 = f32[]{:T(128)} all-reduce(f32[]{:T(128)} %psum.145), channel_id=1, replica_groups=mesh['gz_0'=4,'gz_1'=4,'gz_2'=4,'xy_0'=2,'xy_1'=2] {'gz_1'}, use_global_device_ids=true, to_apply=%region_14.15 | all-reduce | flops 1 | bytes 8 | tf_op jit(solution)/shard_map/psum | solution.py:41
  347.1 6.6 %psum.147 = f32[]{:T(128)} all-reduce(f32[]{:T(128)} %psum.146), channel_id=1, replica_groups=mesh['gz_0'=4,'gz_1'=4,'gz_2'=4,'xy_0'=2,'xy_1'=2] {'gz_2'}, use_global_device_ids=true, to_apply=%region_15.16 | all-reduce | flops 1 | bytes 8 | tf_op jit(solution)/shard_map/psum | solution.py:41
  358.1 11.4 %psum.149 = f32[]{:T(128)} all-reduce(f32[]{:T(128)} %psum.148), channel_id=1, replica_groups=mesh['gz_0'=4,'gz_1'=4,'gz_2'=4,'xy_0'=2,'xy_1'=2] {'xy_1'}, use_global_device_ids=true, to_apply=%region_17.18 | all-reduce | flops 1 | bytes 8 | tf_op jit(solution)/shard_map/psum | solution.py:41
  394.7 27.3 %psum.150 = f32[]{:T(128)} all-reduce(f32[]{:T(128)} %get-tuple-element.32), channel_id=1, replica_groups=mesh['gz_0'=4,'gz_1'=4,'gz_2'=4,'xy_0'=2,'xy_1'=2] {'gz_0'}, use_global_device_ids=true, to_apply=%region_19.20 | all-reduce | flops 1 | bytes 8 | tf_op jit(solution)/shard_map/psum | solution.py:41
  422.0 7.5 %psum.151 = f32[]{:T(128)} all-reduce(f32[]{:T(128)} %psum.150), channel_id=1, replica_groups=mesh['gz_0'=4,'gz_1'=4,'gz_2'=4,'xy_0'=2,'xy_1'=2] {'gz_1'}, use_global_device_ids=true, to_apply=%region_20.21 | all-reduce | flops 1 | bytes 8 | tf_op jit(solution)/shard_map/psum | solution.py:41
  429.5 6.6 %psum.152 = f32[]{:T(128)} all-reduce(f32[]{:T(128)} %psum.151), channel_id=1, replica_groups=mesh['gz_0'=4,'gz_1'=4,'gz_2'=4,'xy_0'=2,'xy_1'=2] {'gz_2'}, use_global_device_ids=true, to_apply=%region_21.22 | all-reduce | flops 1 | bytes 8 | tf_op jit(solution)/shard_map/psum | solution.py:41
  440.5 11.4 %psum.154 = f32[]{:T(128)} all-reduce(f32[]{:T(128)} %psum.153), channel_id=1, replica_groups=mesh['gz_0'=4,'gz_1'=4,'gz_2'=4,'xy_0'=2,'xy_1'=2] {'xy_1'}, use_global_device_ids=true, to_apply=%region_23.24 | all-reduce | flops 1 | bytes 8 | tf_op jit(solution)/shard_map/psum | solution.py:41
  477.1 27.3 %psum.155 = f32[]{:T(128)} all-reduce(f32[]{:T(128)} %get-tuple-element.28), channel_id=1, replica_groups=mesh['gz_0'=4,'gz_1'=4,'gz_2'=4,'xy_0'=2,'xy_1'=2] {'gz_0'}, use_global_device_ids=true, to_apply=%region_25.26 | all-reduce | flops 1 | bytes 8 | tf_op jit(solution)/shard_map/psum | solution.py:41
  505.7 7.5 %psum.156 = f32[]{:T(128)} all-reduce(f32[]{:T(128)} %psum.155), channel_id=1, replica_groups=mesh['gz_0'=4,'gz_1'=4,'gz_2'=4,'xy_0'=2,'xy_1'=2] {'gz_1'}, use_global_device_ids=true, to_apply=%region_26.27 | all-reduce | flops 1 | bytes 8 | tf_op jit(solution)/shard_map/psum | solution.py:41
  514.5 6.6 %psum.157 = f32[]{:T(128)} all-reduce(f32[]{:T(128)} %psum.156), channel_id=1, replica_groups=mesh['gz_0'=4,'gz_1'=4,'gz_2'=4,'xy_0'=2,'xy_1'=2] {'gz_2'}, use_global_device_ids=true, to_apply=%region_27.28 | all-reduce | flops 1 | bytes 8 | tf_op jit(solution)/shard_map/psum | solution.py:41
  530.1 11.6 %psum.159 = f32[]{:T(128)} all-reduce(f32[]{:T(128)} %psum.158), channel_id=1, replica_groups=mesh['gz_0'=4,'gz_1'=4,'gz_2'=4,'xy_0'=2,'xy_1'=2] {'xy_1'}, use_global_device_ids=true, to_apply=%region_29.30 | all-reduce | flops 1 | bytes 8 | tf_op jit(solution)/shard_map/psum | solution.py:41
  (311 shorter events, 213.1 us)
Async XLA Ops:
  0.6 128.1 %collective-permute-start.13 = (bf16[1,2,16,128,128]{4,3,2,1,0:T(8,128)(2,1)}, bf16[1,2,16,128,128]{4,3,2,1,0:T(8,128)(2,1)}, u32[]{:S(2)}, u32[]{:S(2)}) collective-permute-start(bf16[1,2,16,128,128]{4,3,2,1,0:T(8,128)(2,1)} %param.4), channel_id=1, source_target_pairs={{12,0},{16,4},{20,8},{24,12},{28,16},{32,20},{36,24},{40,28},{44,3... | collective-permute-start | bytes 3145736 | tf_op jit(solution)/shard_map/ppermute | solution.py:23
  2.1 130.6 %collective-permute-start.8 = (bf16[1,2,16,128,128]{4,3,2,1,0:T(8,128)(2,1)}, bf16[1,2,16,128,128]{4,3,2,1,0:T(8,128)(2,1)}, u32[]{:S(2)}, u32[]{:S(2)}) collective-permute-start(bf16[1,2,16,128,128]{4,3,2,1,0:T(8,128)(2,1)} %param.4), channel_id=1, source_target_pairs={{8,0},{12,4},{16,8},{20,12},{24,16},{28,20},{32,24},{36,28},{40,32... | collective-permute-start | bytes 3145736 | tf_op jit(solution)/shard_map/ppermute | solution.py:23
  4.8 75.7 %collective-permute-start.2 = (bf16[2,1,32,256]{3,2,1,0:T(8,128)(2,1)}, bf16[2,1,32,256]{3,2,1,0:T(8,128)(2,1)}, u32[]{:S(2)}, u32[]{:S(2)}) collective-permute-start(bf16[2,1,32,256]{3,2,1,0:T(8,128)(2,1)} %convert_element_type.496), channel_id=1, source_target_pairs={{4,0},{8,4},{12,8},{16,12},{20,16},{24,20},{28,24},{32,28},{36,32}... | collective-permute-start | bytes 98312 | tf_op jit(solution)/shard_map/ppermute | solution.py:23
  6.1 75.8 %collective-permute-start.5 = (bf16[2,1,32,256]{3,2,1,0:T(8,128)(2,1)}, bf16[2,1,32,256]{3,2,1,0:T(8,128)(2,1)}, u32[]{:S(2)}, u32[]{:S(2)}) collective-permute-start(bf16[2,1,32,256]{3,2,1,0:T(8,128)(2,1)} %convert_element_type.496), channel_id=1, source_target_pairs={{0,4},{4,8},{8,12},{12,16},{16,20},{20,24},{24,28},{28,32},{32,36}... | collective-permute-start | bytes 98312 | tf_op jit(solution)/shard_map/ppermute | solution.py:23
  12.1 13.5 %collective-permute-start.4 = (f32[1,2,16]{2,1,0:T(2,128)S(1)}, f32[1,2,16]{2,1,0:T(2,128)S(1)}, u32[]{:S(2)}, u32[]{:S(2)}) collective-permute-start(f32[1,2,16]{2,1,0:T(2,128)S(1)} %get-tuple-element.93), channel_id=1, source_target_pairs={{0,4},{4,8},{8,12},{12,16},{16,20},{20,24},{24,28},{28,32},{32,36}... | collective-permute-start | bytes 392 | tf_op jit(solution)/shard_map/ppermute | solution.py:23
  25.6 10.7 %collective-permute-start.9 = (f32[1,2,16]{2,1,0:T(2,128)S(1)}, f32[1,2,16]{2,1,0:T(2,128)S(1)}, u32[]{:S(2)}, u32[]{:S(2)}) collective-permute-start(f32[1,2,16]{2,1,0:T(2,128)S(1)} %get-tuple-element.92), channel_id=1, source_target_pairs={{0,8},{4,12},{8,16},{12,20},{16,24},{20,28},{24,32},{28,36},{32,40... | collective-permute-start | bytes 392 | tf_op jit(solution)/shard_map/ppermute | solution.py:23
  43.4 30.2 %collective-permute-start = (bf16[2,1,1,256]{3,2,1,0:T(2,128)(2,1)S(1)}, bf16[2,1,1,256]{3,2,1,0:T(2,128)(2,1)S(1)}, u32[]{:S(2)}, u32[]{:S(2)}) collective-permute-start(bf16[2,1,1,256]{3,2,1,0:T(2,128)(2,1)S(1)} %get-tuple-element.82), channel_id=1, source_target_pairs={{0,1},{1,2},{2,3},{4,5},{5,6},{6,7},{8,9},{9,10},{10,11},{12,13},{... | collective-permute-start | bytes 3080 | tf_op jit(solution)/shard_map/ppermute | solution.py:31
  79.3 57.2 %collective-permute-start.3 = (bf16[1,2,16,128,128]{4,3,2,1,0:T(8,128)(2,1)S(1)}, bf16[1,2,16,128,128]{4,3,2,1,0:T(8,128)(2,1)S(1)}, u32[]{:S(2)}, u32[]{:S(2)}) collective-permute-start(bf16[1,2,16,128,128]{4,3,2,1,0:T(8,128)(2,1)S(1)} %copy-done.7), channel_id=1, source_target_pairs={{4,0},{8,4},{12,8},{16,12},{20,16},{24,20},{28,24},{32,28},{36,32}... | collective-permute-start | bytes 3145736 | tf_op jit(solution)/shard_map/ppermute | solution.py:23
  80.6 41.8 %collective-permute-start.7 = (bf16[2,1,32,256]{3,2,1,0:T(8,128)(2,1)}, bf16[2,1,32,256]{3,2,1,0:T(8,128)(2,1)}, u32[]{:S(2)}, u32[]{:S(2)}) collective-permute-start(bf16[2,1,32,256]{3,2,1,0:T(8,128)(2,1)} %collective-permute-done.2), channel_id=1, source_target_pairs={{4,0},{8,4},{12,8},{16,12},{20,16},{24,20},{28,24},{32,28},{36,32}... | collective-permute-start | bytes 98312 | tf_op jit(solution)/shard_map/ppermute | solution.py:23
  81.9 41.8 %collective-permute-start.10 = (bf16[2,1,32,256]{3,2,1,0:T(8,128)(2,1)}, bf16[2,1,32,256]{3,2,1,0:T(8,128)(2,1)}, u32[]{:S(2)}, u32[]{:S(2)}) collective-permute-start(bf16[2,1,32,256]{3,2,1,0:T(8,128)(2,1)} %collective-permute-done.5), channel_id=1, source_target_pairs={{0,4},{4,8},{8,12},{12,16},{16,20},{20,24},{24,28},{28,32},{32,36}... | collective-permute-start | bytes 98312 | tf_op jit(solution)/shard_map/ppermute | solution.py:23
  122.4 116.8 %collective-permute-start.12 = (bf16[2,1,32,256]{3,2,1,0:T(8,128)(2,1)}, bf16[2,1,32,256]{3,2,1,0:T(8,128)(2,1)}, u32[]{:S(2)}, u32[]{:S(2)}) collective-permute-start(bf16[2,1,32,256]{3,2,1,0:T(8,128)(2,1)} %collective-permute-done.7), channel_id=1, source_target_pairs={{4,0},{8,4},{12,8},{16,12},{20,16},{24,20},{28,24},{32,28},{36,32}... | collective-permute-start | bytes 98312 | tf_op jit(solution)/shard_map/ppermute | solution.py:23
  123.7 115.5 %collective-permute-start.15 = (bf16[2,1,32,256]{3,2,1,0:T(8,128)(2,1)}, bf16[2,1,32,256]{3,2,1,0:T(8,128)(2,1)}, u32[]{:S(2)}, u32[]{:S(2)}) collective-permute-start(bf16[2,1,32,256]{3,2,1,0:T(8,128)(2,1)} %collective-permute-done.10), channel_id=1, source_target_pairs={{0,4},{4,8},{8,12},{12,16},{16,20},{20,24},{24,28},{28,32},{32,36}... | collective-permute-start | bytes 98312 | tf_op jit(solution)/shard_map/ppermute | solution.py:23
  199.1 38.9 %collective-permute-start.6 = (f32[2,1,2,16]{3,2,1,0:T(2,128)S(1)}, f32[2,1,2,16]{3,2,1,0:T(2,128)S(1)}, u32[]{:S(2)}, u32[]{:S(2)}) collective-permute-start(f32[2,1,2,16]{3,2,1,0:T(2,128)S(1)} %get-tuple-element.97), channel_id=1, source_target_pairs={{0,4},{4,8},{8,12},{12,16},{16,20},{20,24},{24,28},{28,32},{32,36}... | collective-permute-start | bytes 776 | tf_op jit(solution)/shard_map/ppermute | solution.py:23
  207.0 31.4 %collective-permute-start.11 = (f32[2,1,2,16]{3,2,1,0:T(2,128)S(1)}, f32[2,1,2,16]{3,2,1,0:T(2,128)S(1)}, u32[]{:S(2)}, u32[]{:S(2)}) collective-permute-start(f32[2,1,2,16]{3,2,1,0:T(2,128)S(1)} %get-tuple-element.99), channel_id=1, source_target_pairs={{0,8},{4,12},{8,16},{12,20},{16,24},{20,28},{24,32},{28,36},{32,40... | collective-permute-start | bytes 776 | tf_op jit(solution)/shard_map/ppermute | solution.py:23
  298.7 15.1 %collective-permute-start.17 = (bf16[2,1,1,256]{3,2,1,0:T(2,128)(2,1)S(1)}, bf16[2,1,1,256]{3,2,1,0:T(2,128)(2,1)S(1)}, u32[]{:S(2)}, u32[]{:S(2)}) collective-permute-start(bf16[2,1,1,256]{3,2,1,0:T(2,128)(2,1)S(1)} %get-tuple-element.80), channel_id=1, source_target_pairs={{0,1},{1,2},{2,3},{4,5},{5,6},{6,7},{8,9},{9,10},{10,11},{12,13},{... | collective-permute-start | bytes 3080 | tf_op jit(solution)/shard_map/ppermute | solution.py:31
  300.8 12.9 %collective-permute-start.18 = (bf16[2,1,1,256]{3,2,1,0:T(2,128)(2,1)S(1)}, bf16[2,1,1,256]{3,2,1,0:T(2,128)(2,1)S(1)}, u32[]{:S(2)}, u32[]{:S(2)}) collective-permute-start(bf16[2,1,1,256]{3,2,1,0:T(2,128)(2,1)S(1)} %get-tuple-element.81), channel_id=1, source_target_pairs={{1,0},{2,1},{3,2},{5,4},{6,5},{7,6},{9,8},{10,9},{11,10},{13,12},{... | collective-permute-start | bytes 3080 | tf_op jit(solution)/shard_map/ppermute | solution.py:34
  370.3 11.7 %collective-permute-start.27 = (bf16[2,1,32,256]{3,2,1,0:T(8,128)(2,1)S(1)}, bf16[2,1,32,256]{3,2,1,0:T(8,128)(2,1)S(1)}, u32[]{:S(2)}, u32[]{:S(2)}) collective-permute-start(bf16[2,1,32,256]{3,2,1,0:T(8,128)(2,1)S(1)} %get-tuple-element.34), channel_id=1, source_target_pairs={{4,0},{8,4},{12,8},{16,12},{20,16},{24,20},{28,24},{32,28},{36,32}... | collective-permute-start | bytes 98312 | tf_op jit(solution)/shard_map/ppermute | solution.py:23
  371.6 11.7 %collective-permute-start.28 = (bf16[2,1,32,256]{3,2,1,0:T(8,128)(2,1)S(1)}, bf16[2,1,32,256]{3,2,1,0:T(8,128)(2,1)S(1)}, u32[]{:S(2)}, u32[]{:S(2)}) collective-permute-start(bf16[2,1,32,256]{3,2,1,0:T(8,128)(2,1)S(1)} %get-tuple-element.34), channel_id=1, source_target_pairs={{0,4},{4,8},{8,12},{12,16},{16,20},{20,24},{24,28},{28,32},{32,36}... | collective-permute-start | bytes 98312 | tf_op jit(solution)/shard_map/ppermute | solution.py:23
  375.9 17.1 %collective-permute-start.25 = (bf16[2,1,1,256]{3,2,1,0:T(2,128)(2,1)S(1)}, bf16[2,1,1,256]{3,2,1,0:T(2,128)(2,1)S(1)}, u32[]{:S(2)}, u32[]{:S(2)}) collective-permute-start(bf16[2,1,1,256]{3,2,1,0:T(2,128)(2,1)S(1)} %get-tuple-element.78), channel_id=1, source_target_pairs={{0,1},{1,2},{2,3},{4,5},{5,6},{6,7},{8,9},{9,10},{10,11},{12,13},{... | collective-permute-start | bytes 3080 | tf_op jit(solution)/shard_map/ppermute | solution.py:31
  380.0 12.9 %collective-permute-start.26 = (bf16[2,1,1,256]{3,2,1,0:T(2,128)(2,1)S(1)}, bf16[2,1,1,256]{3,2,1,0:T(2,128)(2,1)S(1)}, u32[]{:S(2)}, u32[]{:S(2)}) collective-permute-start(bf16[2,1,1,256]{3,2,1,0:T(2,128)(2,1)S(1)} %get-tuple-element.79), channel_id=1, source_target_pairs={{1,0},{2,1},{3,2},{5,4},{6,5},{7,6},{9,8},{10,9},{11,10},{13,12},{... | collective-permute-start | bytes 3080 | tf_op jit(solution)/shard_map/ppermute | solution.py:34
  452.7 11.7 %collective-permute-start.35 = (bf16[2,1,32,256]{3,2,1,0:T(8,128)(2,1)S(1)}, bf16[2,1,32,256]{3,2,1,0:T(8,128)(2,1)S(1)}, u32[]{:S(2)}, u32[]{:S(2)}) collective-permute-start(bf16[2,1,32,256]{3,2,1,0:T(8,128)(2,1)S(1)} %get-tuple-element.30), channel_id=1, source_target_pairs={{4,0},{8,4},{12,8},{16,12},{20,16},{24,20},{28,24},{32,28},{36,32}... | collective-permute-start | bytes 98312 | tf_op jit(solution)/shard_map/ppermute | solution.py:23
  454.0 11.7 %collective-permute-start.36 = (bf16[2,1,32,256]{3,2,1,0:T(8,128)(2,1)S(1)}, bf16[2,1,32,256]{3,2,1,0:T(8,128)(2,1)S(1)}, u32[]{:S(2)}, u32[]{:S(2)}) collective-permute-start(bf16[2,1,32,256]{3,2,1,0:T(8,128)(2,1)S(1)} %get-tuple-element.30), channel_id=1, source_target_pairs={{0,4},{4,8},{8,12},{12,16},{16,20},{20,24},{24,28},{28,32},{32,36}... | collective-permute-start | bytes 98312 | tf_op jit(solution)/shard_map/ppermute | solution.py:23
  458.2 17.1 %collective-permute-start.33 = (bf16[2,1,1,256]{3,2,1,0:T(2,128)(2,1)S(1)}, bf16[2,1,1,256]{3,2,1,0:T(2,128)(2,1)S(1)}, u32[]{:S(2)}, u32[]{:S(2)}) collective-permute-start(bf16[2,1,1,256]{3,2,1,0:T(2,128)(2,1)S(1)} %get-tuple-element.76), channel_id=1, source_target_pairs={{0,1},{1,2},{2,3},{4,5},{5,6},{6,7},{8,9},{9,10},{10,11},{12,13},{... | collective-permute-start | bytes 3080 | tf_op jit(solution)/shard_map/ppermute | solution.py:31
  462.4 12.9 %collective-permute-start.34 = (bf16[2,1,1,256]{3,2,1,0:T(2,128)(2,1)S(1)}, bf16[2,1,1,256]{3,2,1,0:T(2,128)(2,1)S(1)}, u32[]{:S(2)}, u32[]{:S(2)}) collective-permute-start(bf16[2,1,1,256]{3,2,1,0:T(2,128)(2,1)S(1)} %get-tuple-element.77), channel_id=1, source_target_pairs={{1,0},{2,1},{3,2},{5,4},{6,5},{7,6},{9,8},{10,9},{11,10},{13,12},{... | collective-permute-start | bytes 3080 | tf_op jit(solution)/shard_map/ppermute | solution.py:34
  (40 other events, 705.6 us)
where the time goes:
time: 550 us; the launch traced here: 544 us
  blocking collectives  220 us (40%)
  starting transfers between devices  176 us (32%)
  matrix products  70.1 us (13%)
  waiting for transfers between devices  41 us (7%)
  local copies, waits for them, and re-layouts  17.8 us (3%)
  other arithmetic  13.5 us (2%)
    psum x20, blocking collectives, over_axes(): array = lax.psum(array, axis)  220 us
    ppermute x33, starting transfers between devices, from_behind(): return lax.ppermute(array, axis, pairs)  129 us
    dot_general x22, matrix products, left_product(): jnp.einsum('ja,pak->pjk', table, right, preferred_element_type=jnp.float32)  40.7 us
    ppermute x4, starting transfers between devices, extended(): lax.ppermute(lax.slice_in_dim(block, block.shape[dim] - width, None, axis...  40 us
    ppermute x33, waiting for transfers between devices, from_behind(): return lax.ppermute(array, axis, pairs)  38.2 us
    dot_general x14, matrix products, right_product(): jnp.einsum('pab,bk->pak', left, table, preferred_element_type=jnp.float32)  23.8 us
  transfers between devices with their start and end apart: 41, of which 8 were waited for; matrix products, arithmetic and copies ran while one was open for 16% of the time, Pallas kernels for 0%

commit v1 on v0

--- a/solution.py
+++ b/solution.py
@@ -38,7 +38,7 @@
 
 def over_axes(array, axes):
     for axis in axes:
-        array = lax.psum(array, axis)
+        array = jnp.sum(lax.all_gather(array, axis), axis=0)
     return array
 
 

time: 550 us -> 581 us (1.056)
  local copies, waits for them, and re-layouts: 17.8 us -> 48.7 us
  other arithmetic: 13.5 us -> 25.6 us
  blocking collectives: 220 us -> 208 us
    psum x20 -> x0, blocking collectives: 220 us -> none  [over_axes(): array = lax.psum(array, axis)]
    unnamed x0 -> x20, blocking collectives: none -> 208 us
    unnamed x46 -> x101, local copies, waits for them, and re-layouts: 2.02 us -> 32.9 us
    reduce_sum x0 -> x20, other arithmetic: none -> 12.1 us  [over_axes(): array = jnp.sum(lax.all_gather(array, axis), axis=0)]
  transfers between devices with their start and end apart: 41 -> 41, of which waited for: 8 -> 7; matrix products, arithmetic and copies ran while one was open for 16% -> 15% of each run, Pallas kernels for 0% -> 0%
where the time goes in v1:
time: 581 us; the launch traced here: 574 us
  blocking collectives  208 us (36%)
  starting transfers between devices  176 us (30%)
  matrix products  70.1 us (12%)
  local copies, waits for them, and re-layouts  48.7 us (8%)
  waiting for transfers between devices  40.6 us (7%)
  other arithmetic  25.6 us (4%)
    unnamed x20, blocking collectives  208 us
    ppermute x33, starting transfers between devices, from_behind(): return lax.ppermute(array, axis, pairs)  129 us
    dot_general x22, matrix products, left_product(): jnp.einsum('ja,pak->pjk', table, right, preferred_element_type=jnp.float32)  40.7 us
    ppermute x4, starting transfers between devices, extended(): lax.ppermute(lax.slice_in_dim(block, block.shape[dim] - width, None, axis...  40 us
    ppermute x33, waiting for transfers between devices, from_behind(): return lax.ppermute(array, axis, pairs)  38.1 us
    unnamed x101, local copies, waits for them, and re-layouts  32.9 us
    dot_general x14, matrix products, right_product(): jnp.einsum('pab,bk->pak', left, table, preferred_element_type=jnp.float32)  23.8 us
    reduce_sum x20, other arithmetic, over_axes(): array = jnp.sum(lax.all_gather(array, axis), axis=0)  12.1 us
  transfers between devices with their start and end apart: 41, of which 7 were waited for; matrix products, arithmetic and copies ran while one was open for 15% of the time, Pallas kernels for 0%

profile of v1, /device:TPU:1, one launch (start us, length us, event | category | flops | bytes accessed | tf_op | source)
XLA Modules:
  0.0 573.9 jit_solution(13149762659760493034)
XLA Ops:
  6.1 5.2 collective-permute-start.5
  25.8 9.8 %collective-permute-start.9 = (f32[1,2,16]{2,1,0:T(2,128)S(1)}, f32[1,2,16]{2,1,0:T(2,128)S(1)}, u32[]{:S(2)}, u32[]{:S(2)}) collective-permute-start(f32[1,2,16]{2,1,0:T(2,128)S(1)} %get-tuple-element.92), channel_id=1, source_target_pairs={{0,8},{4,12},{8,16},{12,20},{16,24},{20,28},{24,32},{28,36},{32,40... | collective-permute-start | bytes 392 | tf_op jit(solution)/shard_map/ppermute | solution.py:23
  36.4 6.4 %collective-permute-start.14 = (f32[1,2,16]{2,1,0:T(2,128)S(1)}, f32[1,2,16]{2,1,0:T(2,128)S(1)}, u32[]{:S(2)}, u32[]{:S(2)}) collective-permute-start(f32[1,2,16]{2,1,0:T(2,128)S(1)} %get-tuple-element.91), channel_id=1, source_target_pairs={{0,12},{4,16},{8,20},{12,24},{16,28},{20,32},{24,36},{28,40},{32,4... | collective-permute-start | bytes 392 | tf_op jit(solution)/shard_map/ppermute | solution.py:23
  43.4 29.5 %collective-permute-start = (bf16[2,1,1,256]{3,2,1,0:T(2,128)(2,1)S(1)}, bf16[2,1,1,256]{3,2,1,0:T(2,128)(2,1)S(1)}, u32[]{:S(2)}, u32[]{:S(2)}) collective-permute-start(bf16[2,1,1,256]{3,2,1,0:T(2,128)(2,1)S(1)} %get-tuple-element.82), channel_id=1, source_target_pairs={{0,1},{1,2},{2,3},{4,5},{5,6},{6,7},{8,9},{9,10},{10,11},{12,13},{... | collective-permute-start | bytes 3080 | tf_op jit(solution)/shard_map/ppermute | solution.py:31
  81.9 6.0 %collective-permute-start.10 = (bf16[2,1,32,256]{3,2,1,0:T(8,128)(2,1)}, bf16[2,1,32,256]{3,2,1,0:T(8,128)(2,1)}, u32[]{:S(2)}, u32[]{:S(2)}) collective-permute-start(bf16[2,1,32,256]{3,2,1,0:T(8,128)(2,1)} %collective-permute-done.5), channel_id=1, source_target_pairs={{0,4},{4,8},{8,12},{12,16},{16,20},{20,24},{24,28},{28,32},{32,36}... | collective-permute-start | bytes 98312 | tf_op jit(solution)/shard_map/ppermute | solution.py:23
  88.4 34.0 %collective-permute-done.7 = bf16[2,1,32,256]{3,2,1,0:T(8,128)(2,1)} collective-permute-done((bf16[2,1,32,256]{3,2,1,0:T(8,128)(2,1)}, bf16[2,1,32,256]{3,2,1,0:T(8,128)(2,1)}, u32[]{:S(2)}, u32[]{:S(2)}) %collective-permute-start.7) | collective-permute-done | bytes 32800 | tf_op jit(solution)/shard_map/ppermute | solution.py:23
  199.1 6.8 %collective-permute-start.6 = (f32[2,1,2,16]{3,2,1,0:T(2,128)S(1)}, f32[2,1,2,16]{3,2,1,0:T(2,128)S(1)}, u32[]{:S(2)}, u32[]{:S(2)}) collective-permute-start(f32[2,1,2,16]{3,2,1,0:T(2,128)S(1)} %get-tuple-element.97), channel_id=1, source_target_pairs={{0,4},{4,8},{8,12},{12,16},{16,20},{20,24},{24,28},{28,32},{32,36}... | collective-permute-start | bytes 776 | tf_op jit(solution)/shard_map/ppermute | solution.py:23
  207.0 25.7 %collective-permute-start.11 = (f32[2,1,2,16]{3,2,1,0:T(2,128)S(1)}, f32[2,1,2,16]{3,2,1,0:T(2,128)S(1)}, u32[]{:S(2)}, u32[]{:S(2)}) collective-permute-start(f32[2,1,2,16]{3,2,1,0:T(2,128)S(1)} %get-tuple-element.99), channel_id=1, source_target_pairs={{0,8},{4,12},{8,16},{12,20},{16,24},{20,28},{24,32},{28,36},{32,40... | collective-permute-start | bytes 776 | tf_op jit(solution)/shard_map/ppermute | solution.py:23
  243.0 19.6 %all-reduce = f32[4]{0:T(128)S(1)} all-reduce(f32[4]{0:T(128)S(1)} %dynamic-update-slice), channel_id=1, replica_groups=mesh['gz_0'=4,'gz_1'=4,'gz_2'=4,'xy_0'=2,'xy_1'=2] {'gz_0'}, use_global_device_ids=true, to_apply=%add | all-reduce | flops 4 | bytes 32
  265.3 8.6 %all-reduce.1 = f32[4]{0:T(128)S(1)} all-reduce(f32[4]{0:T(128)S(1)} %dynamic-update-slice.1), channel_id=1, replica_groups=mesh['gz_0'=4,'gz_1'=4,'gz_2'=4,'xy_0'=2,'xy_1'=2] {'gz_1'}, use_global_device_ids=true, to_apply=%add.1 | all-reduce | flops 4 | bytes 32
  276.5 6.0 %all-reduce.2 = f32[4]{0:T(128)S(1)} all-reduce(f32[4]{0:T(128)S(1)} %dynamic-update-slice.2), channel_id=1, replica_groups=mesh['gz_0'=4,'gz_1'=4,'gz_2'=4,'xy_0'=2,'xy_1'=2] {'gz_2'}, use_global_device_ids=true, to_apply=%add.2 | all-reduce | flops 4 | bytes 32
  291.1 10.0 %all-reduce.4 = f32[2]{0:T(128)S(1)} all-reduce(f32[2]{0:T(128)S(1)} %dynamic-update-slice.4), channel_id=1, replica_groups=mesh['gz_0'=4,'gz_1'=4,'gz_2'=4,'xy_0'=2,'xy_1'=2] {'xy_1'}, use_global_device_ids=true, to_apply=%add.4 | all-reduce | flops 2 | bytes 16
  326.3 23.5 %all-reduce.5 = f32[4]{0:T(128)S(1)} all-reduce(f32[4]{0:T(128)S(1)} %dynamic-update-slice.5), channel_id=1, replica_groups=mesh['gz_0'=4,'gz_1'=4,'gz_2'=4,'xy_0'=2,'xy_1'=2] {'gz_0'}, use_global_device_ids=true, to_apply=%add.5 | all-reduce | flops 4 | bytes 32
  351.8 6.9 %all-reduce.6 = f32[4]{0:T(128)S(1)} all-reduce(f32[4]{0:T(128)S(1)} %dynamic-update-slice.6), channel_id=1, replica_groups=mesh['gz_0'=4,'gz_1'=4,'gz_2'=4,'xy_0'=2,'xy_1'=2] {'gz_1'}, use_global_device_ids=true, to_apply=%add.6 | all-reduce | flops 4 | bytes 32
  360.7 6.0 %all-reduce.7 = f32[4]{0:T(128)S(1)} all-reduce(f32[4]{0:T(128)S(1)} %dynamic-update-slice.7), channel_id=1, replica_groups=mesh['gz_0'=4,'gz_1'=4,'gz_2'=4,'xy_0'=2,'xy_1'=2] {'gz_2'}, use_global_device_ids=true, to_apply=%add.7 | all-reduce | flops 4 | bytes 32
  374.4 10.8 %all-reduce.9 = f32[2]{0:T(128)S(1)} all-reduce(f32[2]{0:T(128)S(1)} %dynamic-update-slice.9), channel_id=1, replica_groups=mesh['gz_0'=4,'gz_1'=4,'gz_2'=4,'xy_0'=2,'xy_1'=2] {'xy_1'}, use_global_device_ids=true, to_apply=%add.9 | all-reduce | flops 2 | bytes 16
  412.4 26.7 %all-reduce.10 = f32[4]{0:T(128)S(1)} all-reduce(f32[4]{0:T(128)S(1)} %dynamic-update-slice.10), channel_id=1, replica_groups=mesh['gz_0'=4,'gz_1'=4,'gz_2'=4,'xy_0'=2,'xy_1'=2] {'gz_0'}, use_global_device_ids=true, to_apply=%add.10 | all-reduce | flops 4 | bytes 32
  441.1 6.9 %all-reduce.11 = f32[4]{0:T(128)S(1)} all-reduce(f32[4]{0:T(128)S(1)} %dynamic-update-slice.11), channel_id=1, replica_groups=mesh['gz_0'=4,'gz_1'=4,'gz_2'=4,'xy_0'=2,'xy_1'=2] {'gz_1'}, use_global_device_ids=true, to_apply=%add.11 | all-reduce | flops 4 | bytes 32
  450.0 6.0 %all-reduce.12 = f32[4]{0:T(128)S(1)} all-reduce(f32[4]{0:T(128)S(1)} %dynamic-update-slice.12), channel_id=1, replica_groups=mesh['gz_0'=4,'gz_1'=4,'gz_2'=4,'xy_0'=2,'xy_1'=2] {'gz_2'}, use_global_device_ids=true, to_apply=%add.12 | all-reduce | flops 4 | bytes 32
  463.6 10.8 %all-reduce.14 = f32[2]{0:T(128)S(1)} all-reduce(f32[2]{0:T(128)S(1)} %dynamic-update-slice.14), channel_id=1, replica_groups=mesh['gz_0'=4,'gz_1'=4,'gz_2'=4,'xy_0'=2,'xy_1'=2] {'xy_1'}, use_global_device_ids=true, to_apply=%add.14 | all-reduce | flops 2 | bytes 16
  501.6 26.7 %all-reduce.15 = f32[4]{0:T(128)S(1)} all-reduce(f32[4]{0:T(128)S(1)} %dynamic-update-slice.15), channel_id=1, replica_groups=mesh['gz_0'=4,'gz_1'=4,'gz_2'=4,'xy_0'=2,'xy_1'=2] {'gz_0'}, use_global_device_ids=true, to_apply=%add.15 | all-reduce | flops 4 | bytes 32
  531.5 6.9 %all-reduce.16 = f32[4]{0:T(128)S(1)} all-reduce(f32[4]{0:T(128)S(1)} %dynamic-update-slice.16), channel_id=1, replica_groups=mesh['gz_0'=4,'gz_1'=4,'gz_2'=4,'xy_0'=2,'xy_1'=2] {'gz_1'}, use_global_device_ids=true, to_apply=%add.16 | all-reduce | flops 4 | bytes 32
  541.8 6.1 %all-reduce.17 = f32[4]{0:T(128)S(1)} all-reduce(f32[4]{0:T(128)S(1)} %dynamic-update-slice.17), channel_id=1, replica_groups=mesh['gz_0'=4,'gz_1'=4,'gz_2'=4,'xy_0'=2,'xy_1'=2] {'gz_2'}, use_global_device_ids=true, to_apply=%add.17 | all-reduce | flops 4 | bytes 32
  560.1 11.0 %all-reduce.19 = f32[2]{0:T(128)S(1)} all-reduce(f32[2]{0:T(128)S(1)} %dynamic-update-slice.19), channel_id=1, replica_groups=mesh['gz_0'=4,'gz_1'=4,'gz_2'=4,'xy_0'=2,'xy_1'=2] {'xy_1'}, use_global_device_ids=true, to_apply=%add.19 | all-reduce | flops 2 | bytes 16
  (386 shorter events, 253.3 us)
Async XLA Ops:
  0.6 128.1 %collective-permute-start.13 = (bf16[1,2,16,128,128]{4,3,2,1,0:T(8,128)(2,1)}, bf16[1,2,16,128,128]{4,3,2,1,0:T(8,128)(2,1)}, u32[]{:S(2)}, u32[]{:S(2)}) collective-permute-start(bf16[1,2,16,128,128]{4,3,2,1,0:T(8,128)(2,1)} %param.4), channel_id=1, source_target_pairs={{12,0},{16,4},{20,8},{24,12},{28,16},{32,20},{36,24},{40,28},{44,3... | collective-permute-start | bytes 3145736 | tf_op jit(solution)/shard_map/ppermute | solution.py:23
  2.1 130.6 %collective-permute-start.8 = (bf16[1,2,16,128,128]{4,3,2,1,0:T(8,128)(2,1)}, bf16[1,2,16,128,128]{4,3,2,1,0:T(8,128)(2,1)}, u32[]{:S(2)}, u32[]{:S(2)}) collective-permute-start(bf16[1,2,16,128,128]{4,3,2,1,0:T(8,128)(2,1)} %param.4), channel_id=1, source_target_pairs={{8,0},{12,4},{16,8},{20,12},{24,16},{28,20},{32,24},{36,28},{40,32... | collective-permute-start | bytes 3145736 | tf_op jit(solution)/shard_map/ppermute | solution.py:23
  4.8 75.7 %collective-permute-start.2 = (bf16[2,1,32,256]{3,2,1,0:T(8,128)(2,1)}, bf16[2,1,32,256]{3,2,1,0:T(8,128)(2,1)}, u32[]{:S(2)}, u32[]{:S(2)}) collective-permute-start(bf16[2,1,32,256]{3,2,1,0:T(8,128)(2,1)} %convert_element_type.496), channel_id=1, source_target_pairs={{4,0},{8,4},{12,8},{16,12},{20,16},{24,20},{28,24},{32,28},{36,32}... | collective-permute-start | bytes 98312 | tf_op jit(solution)/shard_map/ppermute | solution.py:23
  6.1 75.8 %collective-permute-start.5 = (bf16[2,1,32,256]{3,2,1,0:T(8,128)(2,1)}, bf16[2,1,32,256]{3,2,1,0:T(8,128)(2,1)}, u32[]{:S(2)}, u32[]{:S(2)}) collective-permute-start(bf16[2,1,32,256]{3,2,1,0:T(8,128)(2,1)} %convert_element_type.496), channel_id=1, source_target_pairs={{0,4},{4,8},{8,12},{12,16},{16,20},{20,24},{24,28},{28,32},{32,36}... | collective-permute-start | bytes 98312 | tf_op jit(solution)/shard_map/ppermute | solution.py:23
  12.1 13.7 %collective-permute-start.4 = (f32[1,2,16]{2,1,0:T(2,128)S(1)}, f32[1,2,16]{2,1,0:T(2,128)S(1)}, u32[]{:S(2)}, u32[]{:S(2)}) collective-permute-start(f32[1,2,16]{2,1,0:T(2,128)S(1)} %get-tuple-element.93), channel_id=1, source_target_pairs={{0,4},{4,8},{8,12},{12,16},{16,20},{20,24},{24,28},{28,32},{32,36}... | collective-permute-start | bytes 392 | tf_op jit(solution)/shard_map/ppermute | solution.py:23
  25.8 10.6 %collective-permute-start.9 = (f32[1,2,16]{2,1,0:T(2,128)S(1)}, f32[1,2,16]{2,1,0:T(2,128)S(1)}, u32[]{:S(2)}, u32[]{:S(2)}) collective-permute-start(f32[1,2,16]{2,1,0:T(2,128)S(1)} %get-tuple-element.92), channel_id=1, source_target_pairs={{0,8},{4,12},{8,16},{12,20},{16,24},{20,28},{24,32},{28,36},{32,40... | collective-permute-start | bytes 392 | tf_op jit(solution)/shard_map/ppermute | solution.py:23
  43.4 30.4 %collective-permute-start = (bf16[2,1,1,256]{3,2,1,0:T(2,128)(2,1)S(1)}, bf16[2,1,1,256]{3,2,1,0:T(2,128)(2,1)S(1)}, u32[]{:S(2)}, u32[]{:S(2)}) collective-permute-start(bf16[2,1,1,256]{3,2,1,0:T(2,128)(2,1)S(1)} %get-tuple-element.82), channel_id=1, source_target_pairs={{0,1},{1,2},{2,3},{4,5},{5,6},{6,7},{8,9},{9,10},{10,11},{12,13},{... | collective-permute-start | bytes 3080 | tf_op jit(solution)/shard_map/ppermute | solution.py:31
  79.3 57.2 %collective-permute-start.3 = (bf16[1,2,16,128,128]{4,3,2,1,0:T(8,128)(2,1)S(1)}, bf16[1,2,16,128,128]{4,3,2,1,0:T(8,128)(2,1)S(1)}, u32[]{:S(2)}, u32[]{:S(2)}) collective-permute-start(bf16[1,2,16,128,128]{4,3,2,1,0:T(8,128)(2,1)S(1)} %copy-done.7), channel_id=1, source_target_pairs={{4,0},{8,4},{12,8},{16,12},{20,16},{24,20},{28,24},{32,28},{36,32}... | collective-permute-start | bytes 3145736 | tf_op jit(solution)/shard_map/ppermute | solution.py:23
  80.6 41.8 %collective-permute-start.7 = (bf16[2,1,32,256]{3,2,1,0:T(8,128)(2,1)}, bf16[2,1,32,256]{3,2,1,0:T(8,128)(2,1)}, u32[]{:S(2)}, u32[]{:S(2)}) collective-permute-start(bf16[2,1,32,256]{3,2,1,0:T(8,128)(2,1)} %collective-permute-done.2), channel_id=1, source_target_pairs={{4,0},{8,4},{12,8},{16,12},{20,16},{24,20},{28,24},{32,28},{36,32}... | collective-permute-start | bytes 98312 | tf_op jit(solution)/shard_map/ppermute | solution.py:23
  81.9 41.8 %collective-permute-start.10 = (bf16[2,1,32,256]{3,2,1,0:T(8,128)(2,1)}, bf16[2,1,32,256]{3,2,1,0:T(8,128)(2,1)}, u32[]{:S(2)}, u32[]{:S(2)}) collective-permute-start(bf16[2,1,32,256]{3,2,1,0:T(8,128)(2,1)} %collective-permute-done.5), channel_id=1, source_target_pairs={{0,4},{4,8},{8,12},{12,16},{16,20},{20,24},{24,28},{28,32},{32,36}... | collective-permute-start | bytes 98312 | tf_op jit(solution)/shard_map/ppermute | solution.py:23
  122.4 117.0 %collective-permute-start.12 = (bf16[2,1,32,256]{3,2,1,0:T(8,128)(2,1)}, bf16[2,1,32,256]{3,2,1,0:T(8,128)(2,1)}, u32[]{:S(2)}, u32[]{:S(2)}) collective-permute-start(bf16[2,1,32,256]{3,2,1,0:T(8,128)(2,1)} %collective-permute-done.7), channel_id=1, source_target_pairs={{4,0},{8,4},{12,8},{16,12},{20,16},{24,20},{28,24},{32,28},{36,32}... | collective-permute-start | bytes 98312 | tf_op jit(solution)/shard_map/ppermute | solution.py:23
  123.7 115.7 %collective-permute-start.15 = (bf16[2,1,32,256]{3,2,1,0:T(8,128)(2,1)}, bf16[2,1,32,256]{3,2,1,0:T(8,128)(2,1)}, u32[]{:S(2)}, u32[]{:S(2)}) collective-permute-start(bf16[2,1,32,256]{3,2,1,0:T(8,128)(2,1)} %collective-permute-done.10), channel_id=1, source_target_pairs={{0,4},{4,8},{8,12},{12,16},{16,20},{20,24},{24,28},{28,32},{32,36}... | collective-permute-start | bytes 98312 | tf_op jit(solution)/shard_map/ppermute | solution.py:23
  199.1 39.1 %collective-permute-start.6 = (f32[2,1,2,16]{3,2,1,0:T(2,128)S(1)}, f32[2,1,2,16]{3,2,1,0:T(2,128)S(1)}, u32[]{:S(2)}, u32[]{:S(2)}) collective-permute-start(f32[2,1,2,16]{3,2,1,0:T(2,128)S(1)} %get-tuple-element.97), channel_id=1, source_target_pairs={{0,4},{4,8},{8,12},{12,16},{16,20},{20,24},{24,28},{28,32},{32,36}... | collective-permute-start | bytes 776 | tf_op jit(solution)/shard_map/ppermute | solution.py:23
  207.0 31.6 %collective-permute-start.11 = (f32[2,1,2,16]{3,2,1,0:T(2,128)S(1)}, f32[2,1,2,16]{3,2,1,0:T(2,128)S(1)}, u32[]{:S(2)}, u32[]{:S(2)}) collective-permute-start(f32[2,1,2,16]{3,2,1,0:T(2,128)S(1)} %get-tuple-element.99), channel_id=1, source_target_pairs={{0,8},{4,12},{8,16},{12,20},{16,24},{20,28},{24,32},{28,36},{32,40... | collective-permute-start | bytes 776 | tf_op jit(solution)/shard_map/ppermute | solution.py:23
  308.1 15.1 %collective-permute-start.17 = (bf16[2,1,1,256]{3,2,1,0:T(2,128)(2,1)S(1)}, bf16[2,1,1,256]{3,2,1,0:T(2,128)(2,1)S(1)}, u32[]{:S(2)}, u32[]{:S(2)}) collective-permute-start(bf16[2,1,1,256]{3,2,1,0:T(2,128)(2,1)S(1)} %get-tuple-element.80), channel_id=1, source_target_pairs={{0,1},{1,2},{2,3},{4,5},{5,6},{6,7},{8,9},{9,10},{10,11},{12,13},{... | collective-permute-start | bytes 3080 | tf_op jit(solution)/shard_map/ppermute | solution.py:31
  310.2 12.9 %collective-permute-start.18 = (bf16[2,1,1,256]{3,2,1,0:T(2,128)(2,1)S(1)}, bf16[2,1,1,256]{3,2,1,0:T(2,128)(2,1)S(1)}, u32[]{:S(2)}, u32[]{:S(2)}) collective-permute-start(bf16[2,1,1,256]{3,2,1,0:T(2,128)(2,1)S(1)} %get-tuple-element.81), channel_id=1, source_target_pairs={{1,0},{2,1},{3,2},{5,4},{6,5},{7,6},{9,8},{10,9},{11,10},{13,12},{... | collective-permute-start | bytes 3080 | tf_op jit(solution)/shard_map/ppermute | solution.py:34
  386.5 11.7 %collective-permute-start.27 = (bf16[2,1,32,256]{3,2,1,0:T(8,128)(2,1)S(1)}, bf16[2,1,32,256]{3,2,1,0:T(8,128)(2,1)S(1)}, u32[]{:S(2)}, u32[]{:S(2)}) collective-permute-start(bf16[2,1,32,256]{3,2,1,0:T(8,128)(2,1)S(1)} %get-tuple-element.34), channel_id=1, source_target_pairs={{4,0},{8,4},{12,8},{16,12},{20,16},{24,20},{28,24},{32,28},{36,32}... | collective-permute-start | bytes 98312 | tf_op jit(solution)/shard_map/ppermute | solution.py:23
  387.8 11.7 %collective-permute-start.28 = (bf16[2,1,32,256]{3,2,1,0:T(8,128)(2,1)S(1)}, bf16[2,1,32,256]{3,2,1,0:T(8,128)(2,1)S(1)}, u32[]{:S(2)}, u32[]{:S(2)}) collective-permute-start(bf16[2,1,32,256]{3,2,1,0:T(8,128)(2,1)S(1)} %get-tuple-element.34), channel_id=1, source_target_pairs={{0,4},{4,8},{8,12},{12,16},{16,20},{20,24},{24,28},{28,32},{32,36}... | collective-permute-start | bytes 98312 | tf_op jit(solution)/shard_map/ppermute | solution.py:23
  392.1 17.1 %collective-permute-start.25 = (bf16[2,1,1,256]{3,2,1,0:T(2,128)(2,1)S(1)}, bf16[2,1,1,256]{3,2,1,0:T(2,128)(2,1)S(1)}, u32[]{:S(2)}, u32[]{:S(2)}) collective-permute-start(bf16[2,1,1,256]{3,2,1,0:T(2,128)(2,1)S(1)} %get-tuple-element.78), channel_id=1, source_target_pairs={{0,1},{1,2},{2,3},{4,5},{5,6},{6,7},{8,9},{9,10},{10,11},{12,13},{... | collective-permute-start | bytes 3080 | tf_op jit(solution)/shard_map/ppermute | solution.py:31
  396.3 12.9 %collective-permute-start.26 = (bf16[2,1,1,256]{3,2,1,0:T(2,128)(2,1)S(1)}, bf16[2,1,1,256]{3,2,1,0:T(2,128)(2,1)S(1)}, u32[]{:S(2)}, u32[]{:S(2)}) collective-permute-start(bf16[2,1,1,256]{3,2,1,0:T(2,128)(2,1)S(1)} %get-tuple-element.79), channel_id=1, source_target_pairs={{1,0},{2,1},{3,2},{5,4},{6,5},{7,6},{9,8},{10,9},{11,10},{13,12},{... | collective-permute-start | bytes 3080 | tf_op jit(solution)/shard_map/ppermute | solution.py:34
  475.8 11.7 %collective-permute-start.35 = (bf16[2,1,32,256]{3,2,1,0:T(8,128)(2,1)S(1)}, bf16[2,1,32,256]{3,2,1,0:T(8,128)(2,1)S(1)}, u32[]{:S(2)}, u32[]{:S(2)}) collective-permute-start(bf16[2,1,32,256]{3,2,1,0:T(8,128)(2,1)S(1)} %get-tuple-element.30), channel_id=1, source_target_pairs={{4,0},{8,4},{12,8},{16,12},{20,16},{24,20},{28,24},{32,28},{36,32}... | collective-permute-start | bytes 98312 | tf_op jit(solution)/shard_map/ppermute | solution.py:23
  477.1 11.7 %collective-permute-start.36 = (bf16[2,1,32,256]{3,2,1,0:T(8,128)(2,1)S(1)}, bf16[2,1,32,256]{3,2,1,0:T(8,128)(2,1)S(1)}, u32[]{:S(2)}, u32[]{:S(2)}) collective-permute-start(bf16[2,1,32,256]{3,2,1,0:T(8,128)(2,1)S(1)} %get-tuple-element.30), channel_id=1, source_target_pairs={{0,4},{4,8},{8,12},{12,16},{16,20},{20,24},{24,28},{28,32},{32,36}... | collective-permute-start | bytes 98312 | tf_op jit(solution)/shard_map/ppermute | solution.py:23
  481.4 17.1 %collective-permute-start.33 = (bf16[2,1,1,256]{3,2,1,0:T(2,128)(2,1)S(1)}, bf16[2,1,1,256]{3,2,1,0:T(2,128)(2,1)S(1)}, u32[]{:S(2)}, u32[]{:S(2)}) collective-permute-start(bf16[2,1,1,256]{3,2,1,0:T(2,128)(2,1)S(1)} %get-tuple-element.76), channel_id=1, source_target_pairs={{0,1},{1,2},{2,3},{4,5},{5,6},{6,7},{8,9},{9,10},{10,11},{12,13},{... | collective-permute-start | bytes 3080 | tf_op jit(solution)/shard_map/ppermute | solution.py:31
  485.5 12.9 %collective-permute-start.34 = (bf16[2,1,1,256]{3,2,1,0:T(2,128)(2,1)S(1)}, bf16[2,1,1,256]{3,2,1,0:T(2,128)(2,1)S(1)}, u32[]{:S(2)}, u32[]{:S(2)}) collective-permute-start(bf16[2,1,1,256]{3,2,1,0:T(2,128)(2,1)S(1)} %get-tuple-element.77), channel_id=1, source_target_pairs={{1,0},{2,1},{3,2},{5,4},{6,5},{7,6},{9,8},{10,9},{11,10},{13,12},{... | collective-permute-start | bytes 3080 | tf_op jit(solution)/shard_map/ppermute | solution.py:34
  (45 other events, 924.2 us)
